TPU v7x, 256 devices: a 8x8x2 block of a 8x8x16 slice. The times are simulated.
256 devices in a mesh: groups: 2 (over z), elem: 128 (over x, y, core).
Axes of the slice: x: 8, y: 8, z: 2, core: 2. Of those that a mesh axis runs over, the one named last changes fastest.
The devices are a block of a 8x8x16 slice.
Arguments:
- snapshots: float32 [2, 4096, 16384], P(None, ('groups', 'elem')), parts along dimension 1, may hold values from -6 to 6
- delays: float32 [384, 2048], replicated, may hold values from -3 to 3
- element_order: int32 [4096], P('groups'), parts along dimension 0, may hold values from 0 to 2047, each once
- beam_table: int32 [512], P('groups'), parts along dimension 0, may hold values from 0 to 383
- band_len: int32 [8], replicated, may hold values from 1 to 32, 128 in all
Outputs:
- beams: float32 [16384, 2, 512], P('elem', None, 'groups'), parts along dimension 2
- power_db: float32 [8, 512], P(None, 'groups'), parts along dimension 1
There are 2 independent parts, one for each index of `groups`. A program takes and returns all parts, laid end to end along the dimension named above; an argument that names none is the same for every part. Nothing has to cross between parts.
Inputs may be any that keep to these rules, and one draw needn't show every extreme that they name: `element_order`: each of 0 to 2047 appears once. `band_len`: the entries sum to 128.
All inputs are finite; a program needn't handle non-finite values.
Results may differ from a plain program's by a relative error of at most 0.0003.
Values sent between devices are 32-bit elements; how exact they have to be, the bound alone decides.
A program may use at most 128 MiB of HBM per device.

v0:
```python
import functools
import math

import jax
import jax.numpy as jnp
from jax import lax
from jax.sharding import Mesh
from jax.sharding import PartitionSpec as P

ELEM = ("elem_0", "elem_1", "elem_2")
GROUPS_ELEM = ("groups", "elem_0", "elem_1", "elem_2")


epsilon = 1e-06


def one_axis_at_a_time(value, axes):
    return functools.reduce(lax.psum, axes, value)


def band_of(band_len, position, unit_count):
    band_ends = jnp.cumsum(band_len)
    band_index = jnp.sum((band_ends <= position).astype(jnp.int32))
    selector = jnp.arange(band_len.shape[0], dtype=jnp.int32) == band_index
    band_size = jnp.sum(jnp.where(selector, band_len, 0))
    band_start = jnp.sum(jnp.where(selector, band_ends, 0)) - band_size
    frequency = (band_start.astype(jnp.float32) + 0.5 * band_size.astype(jnp.float32)) / float(
        unit_count
    )
    return (frequency, band_size, selector.astype(jnp.float32))


def steering(delays, element_order, beam_table, frequency):
    delay_rows = jnp.take(delays, beam_table, axis=0)
    delay_rows = jnp.take(delay_rows, element_order, axis=1)
    phases = 2.0 * math.pi * frequency * delay_rows
    scaling = float(delays.shape[1]) ** (-0.5)
    cosines = jnp.cos(phases) * scaling
    sines = -jnp.sin(phases) * scaling
    upper_rows = jnp.concatenate([cosines.T, sines.T], axis=1)
    lower_rows = jnp.concatenate([-sines.T, cosines.T], axis=1)
    return jnp.concatenate([upper_rows, lower_rows], axis=0)


def project(arrived, weights):
    columns = arrived.shape[2]
    stacked = arrived.reshape(2 * arrived.shape[1], columns)
    return lax.dot_general(
        stacked,
        weights,
        (((0,), (0,)), ((), ())),
        precision=lax.Precision.HIGHEST,
        preferred_element_type=jnp.float32,
    )


def local(snapshots, delays, element_order, beam_table, band_len):
    unit_count = lax.axis_size(ELEM)
    position = lax.axis_index(ELEM)
    frequency, band_size, selector = band_of(band_len, position, unit_count)
    weights = steering(delays, element_order, beam_table, frequency)
    beam_count = beam_table.shape[0]
    local_elems = snapshots.shape[1]
    unit_cols = snapshots.shape[2] // unit_count
    divided = snapshots.reshape(2, local_elems, unit_count, unit_cols)
    pieces = lax.all_to_all(divided, ELEM, split_axis=2, concat_axis=1, tiled=True)
    formed = project(pieces.reshape(2, pieces.shape[1], pieces.shape[3]), weights)
    column_count = formed.shape[0]
    squares = jnp.sum(formed * formed, axis=0)
    power_mean = (squares[:beam_count] + squares[beam_count:]) / (
        band_size.astype(jnp.float32) * column_count
    )
    partial_value = selector[:, None] * power_mean[None, :]
    summed = one_axis_at_a_time(partial_value, ELEM)
    decibels = 10.0 * jnp.log10(summed + epsilon)
    return (formed.reshape(column_count, 2, beam_count), decibels)


def solution(mesh):
    finer = Mesh(
        mesh.devices.reshape(mesh.shape["groups"], 8, 8, 2),
        ("groups", "elem_0", "elem_1", "elem_2"),
    )
    placed = (P(None, GROUPS_ELEM, None), P(), P("groups"), P("groups"), P())
    return jax.shard_map(
        local,
        mesh=finer,
        in_specs=placed,
        out_specs=(P(ELEM, None, "groups"), P(None, "groups")),
        check_vma=False,
    )
```

profile of v0, /device:TPU:513, one launch (start us, length us, event | category | flops | bytes accessed | tf_op | source)
XLA Modules:
  0.0 141.4 jit_solution(13279070334319970445)
XLA Ops:
  0.6 0.0 copy-start
  0.6 3.3 %copy_bitcast_fusion = f32[2,16,128,128]{3,1,0,2:T(8,128)} fusion(f32[2,16,16384]{2,1,0:T(8,128)} %param.5), kind=kLoop, calls=%fused_computation.10 | loop fusion | bytes 4194304 | tf_op jit(solution)/shard_map/reshape | solution.py:65
  4.0 0.0 copy-start.5
  4.0 0.0 copy-start.4
  4.0 28.3 %all-to-all-start = ((f32[2,16,128,128]{3,1,0,2:T(8,128)}), f32[2,16,128,128]{3,1,0,2:T(8,128)}, u32[]{:S(2)}, u32[]{:S(2)}) async-start(f32[2,16,128,128]{3,1,0,2:T(8,128)} %copy_bitcast_fusion), calls=%async_computation | async-start | bytes 4194304 | tf_op jit(solution)/shard_map/all_to_all | solution.py:66
  32.3 0.0 copy-done.5
  32.3 0.2 reduce-window.9
  32.5 0.6 fusion.10
  33.1 1.3 fusion.11
  36.3 0.0 copy-done.4
  36.3 0.0 copy-done
  36.3 2.7 %gather_fusion = f32[256,2048]{1,0:T(8,128)} fusion(f32[384,2048]{1,0:T(8,128)S(1)} %copy-done, s32[1024]{0:T(1024)S(1)} %pad_clamp_fusion), kind=kCustom, calls=%fused_computation | custom fusion | bytes 4195328 | tf_op jit(solution)/shard_map/jit(_take)/gather | solution.py:34
  39.0 3.1 %broadcast_select_fusion = f32[256,2048]{1,0:T(8,128)} fusion(f32[256,2048]{1,0:T(8,128)} %gather_fusion, pred[256]{0:T(512)(128)(4,1)S(1)} %compare_and_fusion.1), kind=kLoop, calls=%fused_computation.14 | loop fusion | flops 524288 | bytes 4194560 | tf_op jit(solution)/shard_map/jit(_take)/select_n | solution.py:34
  42.2 0.0 copy-start.3
  42.2 2.9 %copy.14 = f32[256,2048]{0,1:T(8,128)} copy(f32[256,2048]{1,0:T(8,128)} %broadcast_select_fusion) | data formatting | bytes 4194304 | tf_op jit(solution)/shard_map/jit(_take)/select_n | solution.py:34
  45.1 0.0 copy-done.3
  45.1 10.1 %gather_fusion.1 = f32[2048,256]{1,0:T(8,128)} fusion(f32[256,2048]{0,1:T(8,128)} %copy.14, s32[2048]{0:T(1024)S(1)} %fusion.9), kind=kCustom, calls=%fused_computation.1 | custom fusion | bytes 4202496 | tf_op jit(solution)/shard_map/jit(_take)/gather | solution.py:35
  55.3 0.6 fusion.12
  55.9 11.1 %fusion.14 = (f32[2048,256]{1,0:T(8,128)}, f32[2048,256]{1,0:T(8,128)}, f32[2048,256]{1,0:T(8,128)}) fusion(f32[2048,256]{1,0:T(8,128)} %gather_fusion.1, pred[2048]{0:T(1024)(128)(4,1)S(1)} %compare_and_fusion, f32[]{:T(128)S(6)} %mul_shard_map.7), kind=kLoop, calls=%fused_computation.34 | loop fusion | flops 3145728 | bytes 8390660 | tf_op jit(solution)/shard_map/neg | solution.py:41
  67.1 16.6 %all-to-all-done = f32[2,16,128,128]{3,1,0,2:T(8,128)} async-done(((f32[2,16,128,128]{3,1,0,2:T(8,128)}), f32[2,16,128,128]{3,1,0,2:T(8,128)}, u32[]{:S(2)}, u32[]{:S(2)}) %all-to-all-start) | async-done | bytes 2097184 | tf_op jit(solution)/shard_map/all_to_all | solution.py:66
  83.7 0.0 copy-start.1
  83.7 0.0 copy-start.2
  83.7 1.9 %copy.16 = f32[2,16,128,128]{3,1,2,0:T(8,128)S(1)} copy(f32[2,16,128,128]{3,1,0,2:T(8,128)} %all-to-all-done) | data formatting | bytes 4194304 | tf_op jit(solution)/shard_map/all_to_all | solution.py:66
  85.6 0.3 copy-done.1
  85.9 0.6 copy-done.2
  86.5 17.1 %fusion.8 = (f32[512]{0:T(512)S(1)}, f32[512,128]{1,0:T(8,128)S(1)}) fusion(f32[4096,128]{1,0:T(8,128)S(1)} %bitcast.23, f32[2048,256]{1,0:T(8,128)} %get-tuple-element.12, f32[2048,256]{1,0:T(8,128)S(1)} %copy-done.1, f32[2048,256]{1,0:T(8,128)S(1)} %copy-done.2), kind=kOutput, calls=%fused_computation.16 | convolution fusion | flops 3227647488 | bytes 8652800 | tf_op jit(solution)/shard_map/dot_general | solution.py:48
  103.6 0.8 copy.17
  104.5 0.1 broadcast_multiply_fusion
  104.6 11.9 %psum.21 = f32[8,256]{1,0:T(8,128)S(1)} all-reduce(f32[8,256]{1,0:T(8,128)S(1)} %broadcast_multiply_fusion), channel_id=1, replica_groups=mesh['groups'=2,'elem_0'=8,'elem_1'=8,'elem_2'=2] {'elem_0'}, use_global_device_ids=true, to_apply=%region_5.6 | all-reduce | flops 2048 | bytes 16384 | tf_op jit(solution)/shard_map/psum | solution.py:18
  116.4 13.7 %psum.22 = f32[8,256]{1,0:T(8,128)S(1)} all-reduce(f32[8,256]{1,0:T(8,128)S(1)} %psum.21), channel_id=1, replica_groups=mesh['groups'=2,'elem_0'=8,'elem_1'=8,'elem_2'=2] {'elem_1'}, use_global_device_ids=true, to_apply=%region_6.7 | all-reduce | flops 2048 | bytes 16384 | tf_op jit(solution)/shard_map/psum | solution.py:18
  130.2 10.6 %psum.23 = f32[8,256]{1,0:T(8,128)S(1)} all-reduce(f32[8,256]{1,0:T(8,128)S(1)} %psum.22), channel_id=1, replica_groups=mesh['groups'=2,'elem_0'=8,'elem_1'=8,'elem_2'=2] {'elem_2'}, use_global_device_ids=true, to_apply=%region_7.8 | all-reduce | flops 2048 | bytes 16384 | tf_op jit(solution)/shard_map/psum | solution.py:18
  140.8 0.6 log_multiply_fusion
  (6 shorter events, 0.0 us)
Async XLA Ops:
  0.6 35.7 %copy-start = (f32[384,2048]{1,0:T(8,128)S(1)}, f32[384,2048]{1,0:T(8,128)}, u32[]{:S(2)}) copy-start(f32[384,2048]{1,0:T(8,128)} %param.6) | copy-start | bytes 9437188
  4.0 28.3 %copy-start.5 = (s32[8]{0:T(128)S(1)}, s32[8]{0:T(128)}, u32[]{:S(2)}) copy-start(s32[8]{0:T(128)} %param.9) | copy-start | bytes 100
  4.0 32.3 %copy-start.4 = (s32[256]{0:T(256)S(1)}, s32[256]{0:T(256)}, u32[]{:S(2)}) copy-start(s32[256]{0:T(256)} %param.8) | copy-start | bytes 3076
  4.0 79.7 %all-to-all-start = ((f32[2,16,128,128]{3,1,0,2:T(8,128)}), f32[2,16,128,128]{3,1,0,2:T(8,128)}, u32[]{:S(2)}, u32[]{:S(2)}) async-start(f32[2,16,128,128]{3,1,0,2:T(8,128)} %copy_bitcast_fusion), calls=%async_computation | async-start | bytes 4194304 | tf_op jit(solution)/shard_map/all_to_all | solution.py:66
  42.2 2.9 %copy-start.3 = (s32[2048]{0:T(1024)S(1)}, s32[2048]{0:T(1024)}, u32[]{:S(2)}) copy-start(s32[2048]{0:T(1024)} %param.7) | copy-start | bytes 24580
  83.7 2.2 %copy-start.1 = (f32[2048,256]{1,0:T(8,128)S(1)}, f32[2048,256]{1,0:T(8,128)}, u32[]{:S(2)}) copy-start(f32[2048,256]{1,0:T(8,128)} %get-tuple-element.10) | copy-start | bytes 6291460
  83.7 2.9 %copy-start.2 = (f32[2048,256]{1,0:T(8,128)S(1)}, f32[2048,256]{1,0:T(8,128)}, u32[]{:S(2)}) copy-start(f32[2048,256]{1,0:T(8,128)} %get-tuple-element.11) | copy-start | bytes 6291460
where the time goes:
time: 142 us; the launch traced here: 141 us
  blocking collectives  36.2 us (25%)
  starting transfers between devices  28.3 us (20%)
  local copies, waits for them, and re-layouts  22.8 us (16%)
  other arithmetic  17.8 us (13%)
  matrix products  17.1 us (12%)
  waiting for transfers between devices  16.6 us (12%)
  between operations  2.65 us (2%)
    psum x3, blocking collectives, one_axis_at_a_time(): return functools.reduce(lax.psum, axes, value)  36.2 us
    all_to_all x1, starting transfers between devices, local(): lax.all_to_all(divided, ELEM, split_axis=2, concat_axis=1, tiled=True)  28.3 us
    dot_general x1, matrix products, project(): lax.dot_general(stacked, weights, (((0,), (0,)), ((), ())), precision=lax...  17.1 us
    all_to_all x1, waiting for transfers between devices, local(): lax.all_to_all(divided, ELEM, split_axis=2, concat_axis=1, tiled=True)  16.6 us
    neg x1, other arithmetic, steering(): lower_rows = jnp.concatenate([-sines.T, cosines.T], axis=1)  11.1 us
    gather x1, local copies, waits for them, and re-layouts, steering(): delay_rows = jnp.take(delay_rows, element_order, axis=1)  10.1 us
    reshape x1, local copies, waits for them, and re-layouts, local(): divided = snapshots.reshape(2, local_elems, unit_count, unit_cols)  3.33 us
    select_n x2, other arithmetic, steering(): delay_rows = jnp.take(delays, beam_table, axis=0)  3.14 us
  transfers between devices with their start and end apart: 1, of which 1 were waited for; matrix products, arithmetic and copies ran while one was open for 23% of the time, Pallas kernels for 0%

commit v1 on v0

v1 whole, which is shorter than its diff:
```python
import functools
import math

import jax
import jax.numpy as jnp
from jax import lax
from jax.experimental import pallas as pl
from jax.experimental.pallas import tpu as pltpu
from jax.sharding import PartitionSpec as P

NX, NY, NC = 8, 8, 2
RING = NX * NC
LANES = 128

epsilon = 1e-06

STEPS = (("A", 4), ("B", 3), ("B", -3), ("A", 2), ("A", -2), ("B", 1), ("B", -1), ("A", 0))
P3, M3, P2, M2, P1, M1, P0, M0 = range(8)

COS = (
    0.9999999890590201,
    -19.739204499453688,
    64.93911745988827,
    -85.45013953077586,
    60.16763095018129,
    -25.96759924584206,
    6.528658157862129,
)
SIN = (
    6.283185302511498,
    -41.341700405316736,
    81.60513138576982,
    -76.70301535347629,
    42.02592698341473,
    -14.899846660399582,
    3.2381375010236435,
)


def horner(coefficients, variable, scale):
    value = jnp.full_like(variable, coefficients[-1] * scale)
    for c in coefficients[-2::-1]:
        value = value * variable + c * scale
    return value


def split3(value):
    first = value.astype(jnp.bfloat16)
    rest = value - first.astype(jnp.float32)
    second = rest.astype(jnp.bfloat16)
    third = (rest - second.astype(jnp.float32)).astype(jnp.bfloat16)
    return first, second, third


def dot(a, b):
    return jnp.dot(a, b, preferred_element_type=jnp.float32)


def kernel(
    elem,
    snap,
    delays,
    order,
    table,
    bands,
    beams_out,
    power_out,
    recv,
    delays_v,
    order_v,
    table_v,
    bands_s,
    freq_s,
    gathered,
    picked,
    weights,
    outs,
    ins,
    row_buf,
    sum_buf,
    send_sem,
    recv_sem,
    local_sem,
    ring_send,
    ring_recv,
    row_sem,
    sum_sem,
):
    me = lax.axis_index(elem)
    x, y, c = me // (NY * NC), (me // NC) % NY, me % NC
    odd = (x + y) % 2
    units = NX * NY * NC
    band_count = bands.shape[0]
    beam_count = table.shape[1]
    dirs, elements = delays.shape
    depth = elements // NX
    own = snap.shape[1] * snap.shape[5]

    def at(px, py, pc):
        return {elem: (px * NY + py) * NC + pc}

    def wrap(v):
        return (v + 2 * NX) % NX

    barrier = pltpu.get_barrier_semaphore()

    def greet(t, carry):
        s = (x * NC + c + t) % RING
        pl.semaphore_signal(barrier, inc=1, device_id=at(s // NC, y, s % NC), device_id_type=pl.DeviceIdType.MESH)
        s = (y * NC + c + t) % RING
        pl.semaphore_signal(barrier, inc=1, device_id=at(x, s // NC, s % NC), device_id_type=pl.DeviceIdType.MESH)
        return carry

    lax.fori_loop(1, RING, greet, 0)

    loads = [
        pltpu.make_async_copy(bands, bands_s, local_sem.at[0]),
        pltpu.make_async_copy(order, order_v, local_sem.at[1]),
        pltpu.make_async_copy(table, table_v, local_sem.at[2]),
        pltpu.make_async_copy(delays, delays_v, local_sem.at[3]),
    ]
    for load in loads:
        load.start()
    pl.semaphore_wait(barrier, 2 * (RING - 1))

    def send(step, path, px, py, pc):
        role, off = STEPS[step]
        src = (px, wrap(py + off), pc) if path == 0 else (wrap(px + off), py, pc)
        slot = (x if path == 0 else y) * NC + c
        return pltpu.make_async_remote_copy(
            src_ref=snap.at[:, :, src[0], src[1], src[2]],
            dst_ref=recv.at[step, slot],
            send_sem=send_sem,
            recv_sem=recv_sem.at[step],
            device_id=at(px, py, pc),
            device_id_type=pl.DeviceIdType.MESH,
        )

    def keep(step, path):
        role, off = STEPS[step]
        src = (x, wrap(y + off), c) if path == 0 else (wrap(x + off), y, c)
        slot = (x if path == 0 else y) * NC + c
        return pltpu.make_async_copy(
            snap.at[:, :, src[0], src[1], src[2]], recv.at[step, slot], recv_sem.at[step]
        )

    for step, (role, off) in enumerate(STEPS):
        for path in (0, 1):
            shift = odd if (role == "A") == (path == 0) else 1 - odd

            @pl.when(shift == 0)
            def _():
                keep(step, path).start()

            @pl.when(shift == 1)
            def _():
                if path == 0:
                    send(step, path, wrap(x + 1), y, c).start()
                else:
                    send(step, path, x, wrap(y + 1), c).start()

            def others(t, carry):
                j, pc = t // NC, (c + t) % NC
                if path == 0:
                    send(step, path, wrap(x + shift + 2 * j), y, pc).start()
                else:
                    send(step, path, x, wrap(y + shift + 2 * j), pc).start()
                return carry

            lax.fori_loop(1, RING // 2, others, 0)

    loads[0].wait()
    ends, total = [], jnp.int32(0)
    for b in range(band_count):
        total = total + bands_s[b]
        ends.append(total)

    def unit_of(role, off):
        first = (x * NY + wrap(y + off)) * NC + c
        second = (wrap(x + off) * NY + y) * NC + c
        even = jnp.where(odd == 0, first, second)
        return even if role == "A" else first + second - even

    for step, (role, off) in enumerate(STEPS):
        unit = unit_of(role, off)
        frequency = jnp.float32(0)
        for b in range(band_count):
            start = ends[b] - bands_s[b]
            inside = jnp.logical_and(start <= unit, unit < ends[b])
            middle = start.astype(jnp.float32) + 0.5 * bands_s[b].astype(jnp.float32)
            frequency = frequency + jnp.where(inside, middle, 0.0)
        freq_s[step] = frequency / float(units)

    loads[1].wait()
    loads[2].wait()
    lane = lax.broadcasted_iota(jnp.int32, (8, depth), 1)
    row_order = jnp.zeros((8, depth), jnp.int32)
    group = NC * own
    for px in range(NX):
        part = jnp.broadcast_to(order_v[0:1, px * depth : (px + 1) * depth], (8, depth))
        part = pltpu.roll(part, (px - y + NX) % NX * group, 1)
        row_order = jnp.where(lane // group == px, part, row_order)
    column_order = jnp.broadcast_to(order_v[0:1, pl.ds(pl.multiple_of(x * depth, depth), depth)], (8, depth))
    order_a = jnp.where(odd == 0, row_order, column_order)
    order_b = row_order + column_order - order_a
    both = jnp.concatenate([order_a, order_b], axis=1)[0:1]

    loads[3].wait()
    gathered[...] = jnp.zeros_like(gathered)
    chunk = 256

    def pick_columns(i, carry):
        base = pl.multiple_of(i * chunk, chunk)
        rows = lax.broadcasted_iota(jnp.int32, (chunk, 2 * depth), 0) + base
        hot = jnp.where(rows == both, 1.0, 0.0).astype(jnp.bfloat16)
        one, two, three = split3(delays_v[:, pl.ds(base, chunk)])
        gathered[...] += dot(one, hot) + dot(two, hot) + dot(three, hot)
        return carry

    lax.fori_loop(0, elements // chunk, pick_columns, 0)
    wide = jnp.broadcast_to(table_v[...], (LANES, beam_count)).astype(jnp.float32)
    wide = jnp.transpose(wide)
    hots = []
    for d in range(0, dirs, LANES):
        column = (lax.broadcasted_iota(jnp.int32, (beam_count, LANES), 1) + d).astype(jnp.float32)
        hots.append(jnp.where(wide == column, 1.0, 0.0).astype(jnp.bfloat16))
    hot = jnp.concatenate(hots, axis=1)
    one, two, three = split3(gathered[...])
    rows = dot(hot, one) + dot(hot, two) + dot(hot, three)
    picked[0] = rows[:, :depth]
    picked[1] = rows[:, depth:]

    scale = float(elements) ** -0.5
    block = 32

    def steer(step, role):
        def body(i, carry):
            at_rows = pl.ds(pl.multiple_of(i * block, block), block)
            turns = freq_s[step] * picked[role, at_rows, :]
            nearest = (turns + 12582912.0) - 12582912.0
            r = turns - nearest
            s = r * r
            cosine = horner(COS, s, scale)
            sine = r * horner(SIN, s, scale)
            for n, value in ((0, cosine), (2, sine)):
                high = value.astype(jnp.bfloat16)
                weights[step, n, at_rows, :] = high
                weights[step, n + 1, at_rows, :] = (value - high.astype(jnp.float32)).astype(jnp.bfloat16)
            return carry

        lax.fori_loop(0, beam_count // block, body, 0)

    for step, (role, off) in enumerate(STEPS):
        steer(step, 0 if role == "A" else 1)

    def partial(step):
        pltpu.make_async_copy(recv.at[step], recv.at[step], recv_sem.at[step]).wait()
        data = jnp.concatenate(
            [recv[step, :, 0].reshape(depth, LANES), recv[step, :, 1].reshape(depth, LANES)], axis=1
        )
        high = data.astype(jnp.bfloat16)
        low = (data - high.astype(jnp.float32)).astype(jnp.bfloat16)
        w = weights.at[step]
        cos_part = dot(w[0], high) + dot(w[1], high) + dot(w[0], low)
        sin_part = dot(w[2], high) + dot(w[3], high) + dot(w[2], low)
        real = cos_part[:, :LANES] + sin_part[:, LANES:]
        imag = cos_part[:, LANES:] - sin_part[:, :LANES]
        return real, imag

    def neighbour(role, by):
        px_a = jnp.where(odd == 0, x, wrap(x + by))
        py_a = jnp.where(odd == 0, wrap(y + by), y)
        px_b = jnp.where(odd == 0, wrap(x + by), x)
        py_b = jnp.where(odd == 0, y, wrap(y + by))
        return at(px_a, py_a, c) if role == "A" else at(px_b, py_b, c)

    def pass_on(step, half, buf):
        role, off = STEPS[step]
        by = 1 if buf in (P3, P2, P1, P0) else -1
        return pltpu.make_async_remote_copy(
            src_ref=outs.at[step, half],
            dst_ref=ins.at[buf, half],
            send_sem=ring_send,
            recv_sem=ring_recv.at[buf, half],
            device_id=neighbour(role, by),
            device_id_type=pl.DeviceIdType.MESH,
        )

    def arrived(buf, half):
        pltpu.make_async_copy(ins.at[buf, half], ins.at[buf, half], ring_recv.at[buf, half]).wait()
        return ins[buf, half]

    def compute(step):
        real, imag = partial(step)
        outs[step, 0] = real
        outs[step, 1] = imag

    sent = 0
    compute(0)
    pass_on(0, 0, P3).start()
    pass_on(0, 1, M3).start()
    compute(1)
    pass_on(1, 1, P2).start()
    compute(2)
    pass_on(2, 0, M2).start()
    compute(3)
    outs[1, 0] += arrived(P3, 0)
    pass_on(1, 0, P2).start()
    outs[2, 1] += arrived(M3, 1)
    pass_on(2, 1, M2).start()
    compute(4)
    for half in (1, 0):
        outs[3, half] += arrived(P2, half)
        pass_on(3, half, P1).start()
        outs[4, 1 - half] += arrived(M2, 1 - half)
        pass_on(4, 1 - half, M1).start()
    compute(5)
    compute(6)
    for half in (1, 0):
        outs[5, half] += arrived(P1, half)
        pass_on(5, half, P0).start()
        outs[6, 1 - half] += arrived(M1, 1 - half)
        pass_on(6, 1 - half, M0).start()
    compute(7)
    squares = jnp.zeros((beam_count, LANES), jnp.float32)
    for half in (1, 0):
        value = outs[7, half] + arrived(P0, half) + arrived(M0, half)
        beams_out[half] = value
        squares = squares + value * value

    unit = unit_of("A", 0)
    size = jnp.float32(0)
    for b in range(band_count):
        inside = jnp.logical_and(ends[b] - bands_s[b] <= unit, unit < ends[b])
        size = size + jnp.where(inside, bands_s[b].astype(jnp.float32), 0.0)
    ones = jnp.full((8, LANES), 1.0, jnp.bfloat16)
    sums = jnp.zeros((8, beam_count), jnp.float32)
    for piece in split3(squares):
        sums = sums + lax.dot_general(ones, piece, (((1,), (1,)), ((), ())), preferred_element_type=jnp.float32)
    mine = sums / jnp.full((8, beam_count), size * float(LANES), jnp.float32)
    slot = y * NC + c
    row_buf[slot] = mine[0:1]

    def row_copy(t):
        s = (slot + t) % RING
        return pltpu.make_async_remote_copy(
            src_ref=row_buf.at[slot],
            dst_ref=row_buf.at[slot],
            send_sem=send_sem,
            recv_sem=row_sem,
            device_id=at(x, s // NC, s % NC),
            device_id_type=pl.DeviceIdType.MESH,
        )

    def start_rows(t, carry):
        row_copy(t).start()
        return carry

    lax.fori_loop(1, RING, start_rows, 0)

    band = lax.broadcasted_iota(jnp.int32, (8, beam_count), 0)
    first, last = jnp.zeros_like(band), jnp.zeros_like(band)
    for b in range(band_count):
        first = jnp.where(band == b, ends[b] - bands_s[b], first)
        last = jnp.where(band == b, ends[b], last)
    pltpu.make_async_copy(
        row_buf.at[pl.ds(0, RING - 1)], row_buf.at[pl.ds(0, RING - 1)], row_sem
    ).wait()
    mean = jnp.zeros((8, beam_count), jnp.float32)
    for s in range(RING):
        u = x * RING + s
        inside = jnp.logical_and(first <= u, u < last)
        mean = mean + jnp.where(inside, jnp.broadcast_to(row_buf[s], (8, beam_count)), 0.0)
    sum_buf[x] = mean

    def sum_copy(t):
        return pltpu.make_async_remote_copy(
            src_ref=sum_buf.at[x],
            dst_ref=sum_buf.at[x],
            send_sem=send_sem,
            recv_sem=sum_sem,
            device_id=at(wrap(x + t), y, c),
            device_id_type=pl.DeviceIdType.MESH,
        )

    def start_sums(t, carry):
        sum_copy(t).start()
        return carry

    lax.fori_loop(1, NX, start_sums, 0)
    pltpu.make_async_copy(
        sum_buf.at[pl.ds(0, NX - 1)], sum_buf.at[pl.ds(0, NX - 1)], sum_sem
    ).wait()
    total = sum_buf[0]
    for s in range(1, NX):
        total = total + sum_buf[s]
    power_out[...] = 10.0 * (jnp.log(total + epsilon) * (1.0 / math.log(10.0)))

    for step in range(7):
        pltpu.make_async_copy(recv.at[step], recv.at[step], send_sem).wait()
    half_ring = recv.at[7, pl.ds(0, RING // 2)]
    pltpu.make_async_copy(half_ring, half_ring, send_sem).wait()
    rows = row_buf.at[pl.ds(0, RING - 1)]
    pltpu.make_async_copy(rows, rows, send_sem).wait()
    rows = sum_buf.at[pl.ds(0, NX - 1)]
    pltpu.make_async_copy(rows, rows, send_sem).wait()
    rows = outs.at[pl.ds(0, 7)]
    pltpu.make_async_copy(rows, rows, ring_send).wait()


def local(elem, snapshots, delays, element_order, beam_table, band_len):
    planes, own, columns = snapshots.shape
    tiles = columns // LANES
    view = snapshots.reshape(planes, own // 8, 8, tiles, LANES).transpose(0, 1, 3, 2, 4)
    view = view.reshape(planes, own // 8, NX, NY, NC, 8, LANES)
    beam_count, elements = beam_table.shape[0], delays.shape[1]
    depth = elements // NX
    unit = (RING, planes, own // 8, 8, LANES)
    formed, decibels = pl.pallas_call(
        functools.partial(kernel, elem),
        out_shape=(
            jax.ShapeDtypeStruct((2, beam_count, LANES), jnp.float32),
            jax.ShapeDtypeStruct((band_len.shape[0], beam_count), jnp.float32),
        ),
        in_specs=[pl.BlockSpec(memory_space=pltpu.HBM)] * 5,
        out_specs=(pl.BlockSpec(memory_space=pltpu.VMEM), pl.BlockSpec(memory_space=pltpu.VMEM)),
        scratch_shapes=[
            pltpu.VMEM((8, *unit), jnp.float32),
            pltpu.VMEM(delays.shape, jnp.float32),
            pltpu.VMEM((1, elements), jnp.int32),
            pltpu.VMEM((1, beam_count), jnp.int32),
            pltpu.SMEM(band_len.shape, jnp.int32),
            pltpu.SMEM((8,), jnp.float32),
            pltpu.VMEM((delays.shape[0], 2 * depth), jnp.float32),
            pltpu.VMEM((2, beam_count, depth), jnp.float32),
            pltpu.VMEM((8, 4, beam_count, depth), jnp.bfloat16),
            pltpu.VMEM((8, 2, beam_count, LANES), jnp.float32),
            pltpu.VMEM((8, 2, beam_count, LANES), jnp.float32),
            pltpu.VMEM((RING, 1, beam_count), jnp.float32),
            pltpu.VMEM((NX, band_len.shape[0], beam_count), jnp.float32),
            pltpu.SemaphoreType.DMA(()),
            pltpu.SemaphoreType.DMA((8,)),
            pltpu.SemaphoreType.DMA((4,)),
            pltpu.SemaphoreType.DMA(()),
            pltpu.SemaphoreType.DMA((8, 2)),
            pltpu.SemaphoreType.DMA(()),
            pltpu.SemaphoreType.DMA(()),
        ],
        compiler_params=pltpu.CompilerParams(
            collective_id=1, has_side_effects=True, vmem_limit_bytes=48 * 1024 * 1024
        ),
    )(view, delays, element_order.reshape(1, elements), beam_table.reshape(1, beam_count), band_len)
    return formed.transpose(2, 0, 1), decibels


def solution(mesh):
    return jax.shard_map(
        functools.partial(local, "elem"),
        mesh=mesh,
        in_specs=(P(None, ("groups", "elem"), None), P(), P("groups"), P("groups"), P()),
        out_specs=(P("elem", None, "groups"), P(None, "groups")),
        check_vma=False,
    )
```

time: 142 us -> 79.5 us (0.56)
  Pallas kernels: 0 us -> 71.7 us
  blocking collectives: 36.2 us -> 0 us
  starting transfers between devices: 28.3 us -> 0 us
  other arithmetic: 17.8 us -> 0 us
  matrix products: 17.1 us -> 0 us
  waiting for transfers between devices: 16.6 us -> 0 us
  local copies, waits for them, and re-layouts: 22.8 us -> 6.94 us
  between operations: 2.65 us -> 0.65 us
    pallas_call x0 -> x1, Pallas kernels: none -> 71.7 us  [local(): pl.pallas_call(functools.partial(kernel, elem), out_shape=(jax.ShapeDtype...]
    psum x3 -> x0, blocking collectives: 36.2 us -> none  [one_axis_at_a_time(): return functools.reduce(lax.psum, axes, value)]
    all_to_all x1 -> x0, starting transfers between devices: 28.3 us -> none  [local(): lax.all_to_all(divided, ELEM, split_axis=2, concat_axis=1, tiled=True)]
    dot_general x1 -> x0, matrix products: 17.1 us -> none  [project(): lax.dot_general(stacked, weights, (((0,), (0,)), ((), ())), precision=lax...]
    all_to_all x1 -> x0, waiting for transfers between devices: 16.6 us -> none  [local(): lax.all_to_all(divided, ELEM, split_axis=2, concat_axis=1, tiled=True)]
    gather x2 -> x0, local copies, waits for them, and re-layouts: 12.9 us -> none  [the longest x1 10.1 us: steering(): delay_rows = jnp.take(delay_rows, element_order, axis=1)]
    neg x1 -> x0, other arithmetic: 11.1 us -> none  [steering(): lower_rows = jnp.concatenate([-sines.T, cosines.T], axis=1)]
    unnamed x13 -> x12, local copies, waits for them, and re-layouts: 1.82 us -> 6.94 us
  transfers between devices with their start and end apart: 1 -> 0, of which waited for: 1 -> 0; matrix products, arithmetic and copies ran while one was open for 23% -> 0% of each run, Pallas kernels for 0% -> 0%
where the time goes in v1:
time: 79.5 us; the launch traced here: 79.3 us
  Pallas kernels  71.7 us (90%)
  local copies, waits for them, and re-layouts  6.94 us (9%)
    pallas_call x1, Pallas kernels, local(): pl.pallas_call(functools.partial(kernel, elem), out_shape=(jax.ShapeDtype...  71.7 us
    unnamed x12, local copies, waits for them, and re-layouts  6.94 us

profile of v1, /device:TPU:513, one launch (start us, length us, event | category | flops | bytes accessed | tf_op | source)
XLA Modules:
  0.0 79.3 jit_solution(13862207959795365382)
XLA Ops:
  0.6 0.0 copy-start
  0.6 1.9 %copy-done = f32[384,2048]{1,0:T(8,128)S(1)} copy-done((f32[384,2048]{1,0:T(8,128)S(1)}, f32[384,2048]{1,0:T(8,128)}, u32[]{:S(2)}) %copy-start) | copy-done | bytes 3145752
  2.5 0.0 copy-start.1
  2.5 1.6 %copy-done.1 = f32[2,16,16384]{2,1,0:T(8,128)S(1)} copy-done((f32[2,16,16384]{2,1,0:T(8,128)S(1)}, f32[2,16,16384]{2,1,0:T(8,128)}, u32[]{:S(2)}) %copy-start.1) | copy-done | bytes 2097176
  4.1 0.0 copy-start.2
  4.1 0.7 copy-done.2
  4.8 0.0 copy-start.3
  4.8 0.7 copy-done.3
  5.5 0.0 copy-start.4
  5.5 0.7 copy-done.4
  6.1 71.7 %shard_map.68 = (f32[2,256,128]{2,1,0:T(8,128)S(1)}, f32[8,256]{1,0:T(8,128)S(1)}) custom-call(f32[2,2,8,8,2,8,128]{6,5,4,3,2,1,0:T(8,128)S(1)} %bitcast.8, f32[384,2048]{1,0:T(8,128)S(1)} %copy-done, s32[1,2048]{1,0:T(1,128)S(1)} %bitcast.10, s32[1,256]{1,0:T(1,128)S(1)} %bitcast.11, s32[8]{0:T(128)S(1)} %copy-done.4), custom_call_target="tpu_custom_call" | custom-call | tf_op jit(solution)/shard_map/pallas_call | solution.py:419
  77.8 0.8 %copy.7 = f32[128,2,256]{2,1,0:T(2,128)} copy(f32[128,2,256]{0,2,1:T(8,128)S(1)} %bitcast.9) | data formatting | bytes 524288
  78.7 0.6 copy.9
Async XLA Ops:
  0.6 1.9 %copy-start = (f32[384,2048]{1,0:T(8,128)S(1)}, f32[384,2048]{1,0:T(8,128)}, u32[]{:S(2)}) copy-start(f32[384,2048]{1,0:T(8,128)} %delays.1) | copy-start | bytes 9437188
  2.5 1.6 %copy-start.1 = (f32[2,16,16384]{2,1,0:T(8,128)S(1)}, f32[2,16,16384]{2,1,0:T(8,128)}, u32[]{:S(2)}) copy-start(f32[2,16,16384]{2,1,0:T(8,128)} %param.5) | copy-start | bytes 6291460
  4.1 0.7 copy-start.2
  4.8 0.7 copy-start.3
  5.5 0.7 copy-start.4

commit v2 on v1

--- a/solution.py
+++ b/solution.py
@@ -16,6 +16,7 @@
 
 STEPS = (("A", 4), ("B", 3), ("B", -3), ("A", 2), ("A", -2), ("B", 1), ("B", -1), ("A", 0))
 P3, M3, P2, M2, P1, M1, P0, M0 = range(8)
+AHEAD = 4
 
 COS = (
     0.9999999890590201,
@@ -144,7 +145,8 @@
             snap.at[:, :, src[0], src[1], src[2]], recv.at[step, slot], recv_sem.at[step]
         )
 
-    for step, (role, off) in enumerate(STEPS):
+    def exchange(step):
+        role, off = STEPS[step]
         for path in (0, 1):
             shift = odd if (role == "A") == (path == 0) else 1 - odd
 
@@ -168,6 +170,9 @@
                 return carry
 
             lax.fori_loop(1, RING // 2, others, 0)
+
+    for step in range(AHEAD):
+        exchange(step)
 
     loads[0].wait()
     ends, total = [], jnp.int32(0)
@@ -295,20 +300,23 @@
         outs[step, 0] = real
         outs[step, 1] = imag
 
-    sent = 0
     compute(0)
     pass_on(0, 0, P3).start()
     pass_on(0, 1, M3).start()
+    exchange(4)
     compute(1)
     pass_on(1, 1, P2).start()
     compute(2)
     pass_on(2, 0, M2).start()
+    exchange(5)
     compute(3)
     outs[1, 0] += arrived(P3, 0)
     pass_on(1, 0, P2).start()
     outs[2, 1] += arrived(M3, 1)
     pass_on(2, 1, M2).start()
+    exchange(6)
     compute(4)
+    exchange(7)
     for half in (1, 0):
         outs[3, half] += arrived(P2, half)
         pass_on(3, half, P1).start()
@@ -416,6 +424,7 @@
     beam_count, elements = beam_table.shape[0], delays.shape[1]
     depth = elements // NX
     unit = (RING, planes, own // 8, 8, LANES)
+    operands = (view, delays, element_order.reshape(1, elements), beam_table.reshape(1, beam_count), band_len)
     formed, decibels = pl.pallas_call(
         functools.partial(kernel, elem),
         out_shape=(
@@ -449,7 +458,7 @@
         compiler_params=pltpu.CompilerParams(
             collective_id=1, has_side_effects=True, vmem_limit_bytes=48 * 1024 * 1024
         ),
-    )(view, delays, element_order.reshape(1, elements), beam_table.reshape(1, beam_count), band_len)
+    )(*(pltpu.with_memory_space_constraint(a, pltpu.HBM) for a in operands))
     return formed.transpose(2, 0, 1), decibels
 
 

time: 79.5 us -> 73.4 us (0.923)
  local copies, waits for them, and re-layouts: 6.94 us -> 1.44 us
    unnamed x12 -> x2, local copies, waits for them, and re-layouts: 6.94 us -> 1.44 us
where the time goes in v2:
time: 73.4 us; the launch traced here: 73.3 us
  Pallas kernels  71.2 us (97%)
  local copies, waits for them, and re-layouts  1.44 us (2%)
    pallas_call x1, Pallas kernels, local(): pl.pallas_call(functools.partial(kernel, elem), out_shape=(jax.ShapeDtype...  71.2 us

profile of v2, /device:TPU:513, one launch (start us, length us, event | category | flops | bytes accessed | tf_op | source)
XLA Modules:
  0.0 73.3 jit_solution(11432271822074118138)
XLA Ops:
  0.6 71.2 %shard_map.68 = (f32[2,256,128]{2,1,0:T(8,128)S(1)}, f32[8,256]{1,0:T(8,128)S(1)}) custom-call(f32[2,2,8,8,2,8,128]{6,5,4,3,2,1,0:T(8,128)} %bitcast.9, f32[384,2048]{1,0:T(8,128)} %delays.1, s32[1,2048]{1,0:T(1,128)} %bitcast.10, s32[1,256]{1,0:T(1,128)} %bitcast.11, s32[8]{0:T(128)} %bands.1), custom_call_target="tpu_custom_call" | custom-call | tf_op jit(solution)/shard_map/pallas_call | solution.py:428
  71.9 0.8 %copy.7 = f32[128,2,256]{2,1,0:T(2,128)} copy(f32[128,2,256]{0,2,1:T(8,128)S(1)} %bitcast.8) | data formatting | bytes 524288
  72.7 0.6 copy.9

commit v3 on v2

--- a/solution.py
+++ b/solution.py
@@ -17,6 +17,7 @@
 STEPS = (("A", 4), ("B", 3), ("B", -3), ("A", 2), ("A", -2), ("B", 1), ("B", -1), ("A", 0))
 P3, M3, P2, M2, P1, M1, P0, M0 = range(8)
 AHEAD = 4
+QUARTERS = 4
 
 COS = (
     0.9999999890590201,
@@ -86,10 +87,12 @@
     ring_recv,
     row_sem,
     sum_sem,
+    ready,
+    go,
 ):
     me = lax.axis_index(elem)
     x, y, c = me // (NY * NC), (me // NC) % NY, me % NC
-    odd = (x + y) % 2
+    odd = (x + y + c) % 2
     units = NX * NY * NC
     band_count = bands.shape[0]
     beam_count = table.shape[1]
@@ -103,16 +106,27 @@
     def wrap(v):
         return (v + 2 * NX) % NX
 
+    lead = c == NC - 1
     barrier = pltpu.get_barrier_semaphore()
 
-    def greet(t, carry):
-        s = (x * NC + c + t) % RING
-        pl.semaphore_signal(barrier, inc=1, device_id=at(s // NC, y, s % NC), device_id_type=pl.DeviceIdType.MESH)
-        s = (y * NC + c + t) % RING
-        pl.semaphore_signal(barrier, inc=1, device_id=at(x, s // NC, s % NC), device_id_type=pl.DeviceIdType.MESH)
-        return carry
-
-    lax.fori_loop(1, RING, greet, 0)
+    def tell(semaphore, target):
+        pl.semaphore_signal(semaphore, inc=1, device_id=target, device_id_type=pl.DeviceIdType.MESH)
+
+    def each_lead(act):
+        @pl.when(lead)
+        def _():
+            def one(t, carry):
+                act(wrap(x + t), wrap(y + t))
+                return carry
+
+            lax.fori_loop(1, NX, one, 0)
+
+    def greet(px, py):
+        tell(barrier, at(px, y, c))
+        tell(barrier, at(x, py, c))
+
+    tell(barrier, at(x, y, NC - 1 - c))
+    each_lead(greet)
 
     loads = [
         pltpu.make_async_copy(bands, bands_s, local_sem.at[0]),
@@ -122,7 +136,21 @@
     ]
     for load in loads:
         load.start()
-    pl.semaphore_wait(barrier, 2 * (RING - 1))
+    pl.semaphore_wait(barrier, jnp.where(lead, 2 * (NX - 1) + 1, 1))
+
+    def pass_ready(px, py):
+        tell(ready.at[0, x], at(px, y, c))
+        tell(ready.at[1, y], at(x, py, c))
+
+    each_lead(pass_ready)
+
+    @pl.when(lead)
+    def _():
+        tell(go, at(x, y, NC - 1 - c))
+
+    @pl.when(jnp.logical_not(lead))
+    def _():
+        pl.semaphore_wait(go, 1)
 
     def send(step, path, px, py, pc):
         role, off = STEPS[step]
@@ -145,35 +173,46 @@
             snap.at[:, :, src[0], src[1], src[2]], recv.at[step, slot], recv_sem.at[step]
         )
 
-    def exchange(step):
+    def exchange(step, pc):
         role, off = STEPS[step]
         for path in (0, 1):
-            shift = odd if (role == "A") == (path == 0) else 1 - odd
-
-            @pl.when(shift == 0)
+            shift = (x + y + pc + (role == "B") + path) % 2
+            mine = jnp.logical_and(shift == 0, c == pc)
+
+            def away(j):
+                by = shift + 2 * j
+                return (wrap(x + by), y) if path == 0 else (x, wrap(y + by))
+
+            @pl.when(mine)
             def _():
                 keep(step, path).start()
 
-            @pl.when(shift == 1)
+            @pl.when(jnp.logical_not(mine))
             def _():
-                if path == 0:
-                    send(step, path, wrap(x + 1), y, c).start()
-                else:
-                    send(step, path, x, wrap(y + 1), c).start()
-
-            def others(t, carry):
-                j, pc = t // NC, (c + t) % NC
-                if path == 0:
-                    send(step, path, wrap(x + shift + 2 * j), y, pc).start()
-                else:
-                    send(step, path, x, wrap(y + shift + 2 * j), pc).start()
+                send(step, path, *away(0), pc).start()
+
+            def others(j, carry):
+                send(step, path, *away(j), pc).start()
                 return carry
 
-            lax.fori_loop(1, RING // 2, others, 0)
+            lax.fori_loop(1, NX // 2, others, 0)
 
     for step in range(AHEAD):
-        exchange(step)
-
+        exchange(step, NC - 1)
+
+    def others_ready(t, carry):
+        for axis, chip in ((0, wrap(x + t)), (1, wrap(y + t))):
+            pl.semaphore_wait(ready.at[axis, chip], 1)
+
+            @pl.when(lead)
+            def _():
+                tell(ready.at[axis, chip], at(x, y, NC - 1 - c))
+
+        return carry
+
+    lax.fori_loop(1, NX, others_ready, 0)
+    for step in range(AHEAD):
+        exchange(step, 0)
     loads[0].wait()
     ends, total = [], jnp.int32(0)
     for b in range(band_count):
@@ -279,62 +318,78 @@
         py_b = jnp.where(odd == 0, y, wrap(y + by))
         return at(px_a, py_a, c) if role == "A" else at(px_b, py_b, c)
 
-    def pass_on(step, half, buf):
+    def pass_on(step, q, buf):
         role, off = STEPS[step]
         by = 1 if buf in (P3, P2, P1, P0) else -1
         return pltpu.make_async_remote_copy(
-            src_ref=outs.at[step, half],
-            dst_ref=ins.at[buf, half],
+            src_ref=outs.at[step, q],
+            dst_ref=ins.at[buf, q],
             send_sem=ring_send,
-            recv_sem=ring_recv.at[buf, half],
+            recv_sem=ring_recv.at[buf, q],
             device_id=neighbour(role, by),
             device_id_type=pl.DeviceIdType.MESH,
         )
 
-    def arrived(buf, half):
-        pltpu.make_async_copy(ins.at[buf, half], ins.at[buf, half], ring_recv.at[buf, half]).wait()
-        return ins[buf, half]
+    def arrived(buf, q):
+        pltpu.make_async_copy(ins.at[buf, q], ins.at[buf, q], ring_recv.at[buf, q]).wait()
+        return ins[buf, q]
+
+    piece = 2 * beam_count // QUARTERS
 
     def compute(step):
         real, imag = partial(step)
-        outs[step, 0] = real
-        outs[step, 1] = imag
-
+        for h, value in enumerate((real, imag)):
+            for q in range(QUARTERS // 2):
+                outs[step, h * (QUARTERS // 2) + q] = value[q * piece : (q + 1) * piece]
+
+    low, high = range(QUARTERS // 2), range(QUARTERS // 2, QUARTERS)
     compute(0)
-    pass_on(0, 0, P3).start()
-    pass_on(0, 1, M3).start()
-    exchange(4)
+    for q in low:
+        pass_on(0, q, P3).start()
+    for q in high:
+        pass_on(0, q, M3).start()
+    for pc in range(NC):
+        exchange(4, pc)
     compute(1)
-    pass_on(1, 1, P2).start()
+    for q in high:
+        pass_on(1, q, P2).start()
     compute(2)
-    pass_on(2, 0, M2).start()
-    exchange(5)
+    for q in low:
+        pass_on(2, q, M2).start()
+    for pc in range(NC):
+        exchange(5, pc)
     compute(3)
-    outs[1, 0] += arrived(P3, 0)
-    pass_on(1, 0, P2).start()
-    outs[2, 1] += arrived(M3, 1)
-    pass_on(2, 1, M2).start()
-    exchange(6)
+    for p, m in zip(low, high):
+        outs[1, p] += arrived(P3, p)
+        pass_on(1, p, P2).start()
+        outs[2, m] += arrived(M3, m)
+        pass_on(2, m, M2).start()
+    for pc in range(NC):
+        exchange(6, pc)
     compute(4)
-    exchange(7)
-    for half in (1, 0):
-        outs[3, half] += arrived(P2, half)
-        pass_on(3, half, P1).start()
-        outs[4, 1 - half] += arrived(M2, 1 - half)
-        pass_on(4, 1 - half, M1).start()
+    for pc in range(NC):
+        exchange(7, pc)
+    up, down = (*high, *low), (*low, *high)
+    for p, m in zip(up, down):
+        outs[3, p] += arrived(P2, p)
+        pass_on(3, p, P1).start()
+        outs[4, m] += arrived(M2, m)
+        pass_on(4, m, M1).start()
     compute(5)
     compute(6)
-    for half in (1, 0):
-        outs[5, half] += arrived(P1, half)
-        pass_on(5, half, P0).start()
-        outs[6, 1 - half] += arrived(M1, 1 - half)
-        pass_on(6, 1 - half, M0).start()
+    for p, m in zip(up, down):
+        outs[5, p] += arrived(P1, p)
+        pass_on(5, p, P0).start()
+        outs[6, m] += arrived(M1, m)
+        pass_on(6, m, M0).start()
     compute(7)
-    squares = jnp.zeros((beam_count, LANES), jnp.float32)
-    for half in (1, 0):
-        value = outs[7, half] + arrived(P0, half) + arrived(M0, half)
-        beams_out[half] = value
-        squares = squares + value * value
+    parts = [jnp.zeros((piece, LANES), jnp.float32) for _ in low]
+    for q in up:
+        value = outs[7, q] + arrived(P0, q) + arrived(M0, q)
+        k = q % len(low)
+        beams_out[q // len(low), k * piece : (k + 1) * piece] = value
+        parts[k] = parts[k] + value * value
+    squares = jnp.concatenate(parts, axis=0)
 
     unit = unit_of("A", 0)
     size = jnp.float32(0)
@@ -443,17 +498,19 @@
             pltpu.VMEM((delays.shape[0], 2 * depth), jnp.float32),
             pltpu.VMEM((2, beam_count, depth), jnp.float32),
             pltpu.VMEM((8, 4, beam_count, depth), jnp.bfloat16),
-            pltpu.VMEM((8, 2, beam_count, LANES), jnp.float32),
-            pltpu.VMEM((8, 2, beam_count, LANES), jnp.float32),
+            pltpu.VMEM((8, QUARTERS, 2 * beam_count // QUARTERS, LANES), jnp.float32),
+            pltpu.VMEM((8, QUARTERS, 2 * beam_count // QUARTERS, LANES), jnp.float32),
             pltpu.VMEM((RING, 1, beam_count), jnp.float32),
             pltpu.VMEM((NX, band_len.shape[0], beam_count), jnp.float32),
             pltpu.SemaphoreType.DMA(()),
             pltpu.SemaphoreType.DMA((8,)),
             pltpu.SemaphoreType.DMA((4,)),
             pltpu.SemaphoreType.DMA(()),
-            pltpu.SemaphoreType.DMA((8, 2)),
+            pltpu.SemaphoreType.DMA((8, QUARTERS)),
             pltpu.SemaphoreType.DMA(()),
             pltpu.SemaphoreType.DMA(()),
+            pltpu.SemaphoreType.REGULAR((2, NX)),
+            pltpu.SemaphoreType.REGULAR,
         ],
         compiler_params=pltpu.CompilerParams(
             collective_id=1, has_side_effects=True, vmem_limit_bytes=48 * 1024 * 1024

time: 73.4 us -> 68.7 us (0.936)
  Pallas kernels: 71.2 us -> 66.5 us
    pallas_call x1, Pallas kernels: 71.2 us -> 66.5 us  [local(): pl.pallas_call(functools.partial(kernel, elem), out_shape=(jax.ShapeDtype...]
where the time goes in v3:
time: 68.7 us; the launch traced here: 68.6 us
  Pallas kernels  66.5 us (97%)
  local copies, waits for them, and re-layouts  1.44 us (2%)
    pallas_call x1, Pallas kernels, local(): pl.pallas_call(functools.partial(kernel, elem), out_shape=(jax.ShapeDtype...  66.5 us
    unnamed x2, local copies, waits for them, and re-layouts  1.44 us

profile of v3, /device:TPU:513, one launch (start us, length us, event | category | flops | bytes accessed | tf_op | source)
XLA Modules:
  0.0 68.6 jit_solution(14704591075483784563)
XLA Ops:
  0.6 66.5 %shard_map.68 = (f32[2,256,128]{2,1,0:T(8,128)S(1)}, f32[8,256]{1,0:T(8,128)S(1)}) custom-call(f32[2,2,8,8,2,8,128]{6,5,4,3,2,1,0:T(8,128)} %bitcast.9, f32[384,2048]{1,0:T(8,128)} %delays.1, s32[1,2048]{1,0:T(1,128)} %bitcast.10, s32[1,256]{1,0:T(1,128)} %bitcast.11, s32[8]{0:T(128)} %bands.1), custom_call_target="tpu_custom_call" | custom-call | tf_op jit(solution)/shard_map/pallas_call | solution.py:483
  67.1 0.8 %copy.7 = f32[128,2,256]{2,1,0:T(2,128)} copy(f32[128,2,256]{0,2,1:T(8,128)S(1)} %bitcast.8) | data formatting | bytes 524288
  68.0 0.6 copy.9

commit v4 on v3

--- a/solution.py
+++ b/solution.py
@@ -16,7 +16,7 @@
 
 STEPS = (("A", 4), ("B", 3), ("B", -3), ("A", 2), ("A", -2), ("B", 1), ("B", -1), ("A", 0))
 P3, M3, P2, M2, P1, M1, P0, M0 = range(8)
-AHEAD = 4
+AHEAD = 7
 QUARTERS = 4
 
 COS = (
@@ -348,33 +348,27 @@
         pass_on(0, q, P3).start()
     for q in high:
         pass_on(0, q, M3).start()
-    for pc in range(NC):
-        exchange(4, pc)
     compute(1)
     for q in high:
         pass_on(1, q, P2).start()
     compute(2)
     for q in low:
         pass_on(2, q, M2).start()
-    for pc in range(NC):
-        exchange(5, pc)
     compute(3)
     for p, m in zip(low, high):
         outs[1, p] += arrived(P3, p)
         pass_on(1, p, P2).start()
         outs[2, m] += arrived(M3, m)
         pass_on(2, m, M2).start()
-    for pc in range(NC):
-        exchange(6, pc)
     compute(4)
-    for pc in range(NC):
-        exchange(7, pc)
     up, down = (*high, *low), (*low, *high)
     for p, m in zip(up, down):
         outs[3, p] += arrived(P2, p)
         pass_on(3, p, P1).start()
         outs[4, m] += arrived(M2, m)
         pass_on(4, m, M1).start()
+    for pc in range(NC):
+        exchange(7, pc)
     compute(5)
     compute(6)
     for p, m in zip(up, down):

time: 68.7 us -> 67.4 us (0.981)
  Pallas kernels: 66.5 us -> 65.2 us
    pallas_call x1, Pallas kernels: 66.5 us -> 65.2 us  [local(): pl.pallas_call(functools.partial(kernel, elem), out_shape=(jax.ShapeDtype...]
where the time goes in v4:
time: 67.4 us; the launch traced here: 67.3 us
  Pallas kernels  65.2 us (97%)
  local copies, waits for them, and re-layouts  1.44 us (2%)
    pallas_call x1, Pallas kernels, local(): pl.pallas_call(functools.partial(kernel, elem), out_shape=(jax.ShapeDtype...  65.2 us
    unnamed x2, local copies, waits for them, and re-layouts  1.44 us

profile of v4, /device:TPU:513, one launch (start us, length us, event | category | flops | bytes accessed | tf_op | source)
XLA Modules:
  0.0 67.3 jit_solution(245026720621568081)
XLA Ops:
  0.6 65.2 %shard_map.68 = (f32[2,256,128]{2,1,0:T(8,128)S(1)}, f32[8,256]{1,0:T(8,128)S(1)}) custom-call(f32[2,2,8,8,2,8,128]{6,5,4,3,2,1,0:T(8,128)} %bitcast.9, f32[384,2048]{1,0:T(8,128)} %delays.1, s32[1,2048]{1,0:T(1,128)} %bitcast.10, s32[1,256]{1,0:T(1,128)} %bitcast.11, s32[8]{0:T(128)} %bands.1), custom_call_target="tpu_custom_call" | custom-call | tf_op jit(solution)/shard_map/pallas_call | solution.py:477
  65.9 0.8 %copy.7 = f32[128,2,256]{2,1,0:T(2,128)} copy(f32[128,2,256]{0,2,1:T(8,128)S(1)} %bitcast.8) | data formatting | bytes 524288
  66.7 0.6 copy.9

commit v5 on v4

--- a/solution.py
+++ b/solution.py
@@ -398,8 +398,11 @@
     slot = y * NC + c
     row_buf[slot] = mine[0:1]
 
+    def far_first(t, length):
+        return length // 2 + jnp.where(t % 2 == 0, t // 2, -(t // 2))
+
     def row_copy(t):
-        s = (slot + t) % RING
+        s = (slot + far_first(t, RING)) % RING
         return pltpu.make_async_remote_copy(
             src_ref=row_buf.at[slot],
             dst_ref=row_buf.at[slot],
@@ -436,7 +439,7 @@
             dst_ref=sum_buf.at[x],
             send_sem=send_sem,
             recv_sem=sum_sem,
-            device_id=at(wrap(x + t), y, c),
+            device_id=at(wrap(x + far_first(t, NX)), y, c),
             device_id_type=pl.DeviceIdType.MESH,
         )
 

time: 67.4 us -> 67.3 us (level)
  no operation moved by 1% of the time
where the time goes in v5:
time: 67.3 us; the launch traced here: 67.2 us
  Pallas kernels  65.1 us (97%)
  local copies, waits for them, and re-layouts  1.44 us (2%)
    pallas_call x1, Pallas kernels, local(): pl.pallas_call(functools.partial(kernel, elem), out_shape=(jax.ShapeDtype...  65.1 us
    unnamed x2, local copies, waits for them, and re-layouts  1.44 us

profile of v5, /device:TPU:513, one launch (start us, length us, event | category | flops | bytes accessed | tf_op | source)
XLA Modules:
  0.0 67.2 jit_solution(17528497092700736814)
XLA Ops:
  0.6 65.1 %shard_map.68 = (f32[2,256,128]{2,1,0:T(8,128)S(1)}, f32[8,256]{1,0:T(8,128)S(1)}) custom-call(f32[2,2,8,8,2,8,128]{6,5,4,3,2,1,0:T(8,128)} %bitcast.9, f32[384,2048]{1,0:T(8,128)} %delays.1, s32[1,2048]{1,0:T(1,128)} %bitcast.10, s32[1,256]{1,0:T(1,128)} %bitcast.11, s32[8]{0:T(128)} %bands.1), custom_call_target="tpu_custom_call" | custom-call | tf_op jit(solution)/shard_map/pallas_call | solution.py:480
  65.7 0.8 %copy.7 = f32[128,2,256]{2,1,0:T(2,128)} copy(f32[128,2,256]{0,2,1:T(8,128)S(1)} %bitcast.8) | data formatting | bytes 524288
  66.6 0.6 copy.9
